TPU v7x, 256 devices: a whole 4x4x8 slice. The times are simulated.
256 devices in a mesh: dp: 64 (over z, y, core), mp: 4 (over x).
Axes of the slice: x: 4, y: 4, z: 8, core: 2. Of those that a mesh axis runs over, the one named last changes fastest.
Arguments:
- sample_inputs: bfloat16 [512, 512], P(('dp', 'mp')), may hold values from -6 to 6
- sample_outputs: bfloat16 [512, 1024], P(('dp', 'mp')), may hold values from -6 to 6
- directions: bfloat16 [512, 256, 512], P(('dp', 'mp')), may hold values from -24 to 24
- jacobian_targets: bfloat16 [512, 256, 1024], P(('dp', 'mp')), may hold values from -24 to 24
- jacobian_ranks: int32 [512], P(('dp', 'mp')), may hold values from 16 to 256, as said below
- encoder_weight: bfloat16 [512, 2048], replicated, may hold values from -0.25 to 0.25
- decoder_weight: bfloat16 [1024, 2048], replicated, may hold values from -0.125 to 0.125
Outputs:
- grad_encoder: float32 [512, 2048], P('dp', 'mp')
- grad_decoder: float32 [1024, 2048], P('dp', 'mp')
Inputs may be any that keep to these rules, and one draw needn't show every extreme that they name: `jacobian_ranks`: every rank is a multiple of 16.
All inputs are finite; a program needn't handle non-finite values.
Results may differ from a plain program's by a relative error of at most 0.0013.
Values may be sent and summed in bfloat16 or wider, within the bound.
No kernel may reach another device: no remote copies, remote signals or barrier semaphores. Data moves between devices by JAX's collectives and lax.ppermute only.
A program may use at most 128 MiB of HBM per device.

v0:
```python
import functools
import math

import jax
import jax.numpy as jnp
from jax import lax
from jax.experimental import pallas as pl
from jax.experimental.pallas import tpu as pltpu
from jax.sharding import PartitionSpec as P


F32 = jnp.float32
BF16 = jnp.bfloat16
S16 = jnp.int16
BLK = 16
EXTRA = 16
COLS = 512
PER = (16, 8)
TOP = 32700.0
TINY = 1e-30
MIB = 1 << 20
SIZES = ((256, 256), (416, 512), (528, 640))
ROWS = 784
RANKS_AT = 512

NN = (((1,), (0,)), ((), ()))
NT = (((1,), (1,)), ((), ()))
VM = pl.BlockSpec(memory_space=pltpu.VMEM)
SM = pl.BlockSpec(memory_space=pltpu.SMEM)
HB = pl.BlockSpec(memory_space=pltpu.HBM)


def dot(a, b, dims=NN):
    return lax.dot_general(a, b, dims, preferred_element_type=F32)


def section_base(sections, index):
    return sum(PER[p] * n for p, n in sections[:index])


def message(sections):
    rows = -(-section_base(sections, len(sections)) // 16) * 16 + 16
    return jax.ShapeDtypeStruct((rows, COLS), S16)


def exponents(largest):
    return jnp.floor(jnp.log(jnp.maximum(largest, TINY)) * (1.0 / math.log(2.0))) + 1.0


def power(e):
    return jnp.exp(e * math.log(2.0))


def tall(v, rows):
    return jnp.concatenate([v] * (rows // 8), axis=0) if rows > 8 else v


def coded(x, mult):
    return jnp.round(x * tall(mult, x.shape[0])).astype(jnp.int32).astype(S16)


def plain(q, mult):
    return q.astype(jnp.int32).astype(F32) * tall(mult, q.shape[0])


def fold_max(best, x):
    for r in range(0, x.shape[0], 8):
        best = jnp.maximum(best, jnp.abs(x[r : r + 8]))
    return best


def write_scales(msg, best):
    es = [exponents(b) for b in best]
    last = jnp.concatenate([es[0], es[-1]], axis=0).astype(jnp.int32).astype(S16)
    msg[msg.shape[0] - 16 :, :] = last
    return [power(-e) * TOP for e in es]


def read_scales(msg):
    e = msg[msg.shape[0] - 16 :, :].astype(jnp.int32).astype(F32)
    s = power(e) * (1.0 / TOP)
    return s[0:8], s[8:16]


def rows_loop(count, step, body, init):
    n = count // step
    if n == 1:
        return body(0, init)
    unroll = 4 if n % 4 == 0 else (2 if n % 2 == 0 else 1)

    def it(i, carry):
        for u in range(unroll):
            carry = body(pl.multiple_of((i * unroll + u) * step, step), carry)
        return carry

    return lax.fori_loop(0, n // unroll, it, init)


def encode_rows(src, src_start, count, msg, msg_start, mult):
    def body(o, carry):
        msg[pl.ds(msg_start + o, 16), :] = coded(src[pl.ds(src_start + o, 16), :], mult)
        return carry

    rows_loop(count, 16, body, 0)


def step_kernel(state_parts, parts, groups, ins, outs, *refs):
    ns, np_ = len(state_parts), len(parts)
    states, msgs = refs[:ns], refs[ns : ns + len(ins)]
    rest = refs[ns + len(ins) :]
    news = dict(zip(parts, rest[:np_]))
    sent = rest[np_ : np_ + len(outs)]
    holds = dict(zip(parts, rest[np_ + len(outs) :]))
    scales = [read_scales(m) for m in msgs]
    best = [[jnp.zeros((8, COLS), F32)] * len(o) for o in outs]
    pending = []
    held = {p: 0 for p in parts}
    for index, start, blocks, arrived, dest in groups:
        part = state_parts[index]
        per = PER[part]
        count = per * blocks
        step = min(16, count)

        def value(o, index=index, part=part, per=per, start=start, arrived=arrived, step=step):
            x = states[index][pl.ds(start * per + o, step), :]
            for m, at in arrived:
                where = [p for p, _ in ins[m]].index(part)
                base = section_base(ins[m], where) + per * at
                x = x + plain(msgs[m][pl.ds(base + o, step), :], scales[m][where])
            return x

        if dest[0] == "keep":

            def body(o, carry, value=value, part=part, to=dest[1] * per, step=step):
                news[part][pl.ds(to + o, step), :] = value(o)
                return carry

            rows_loop(count, step, body, 0)
        else:
            where = [p for p, _ in outs[dest[1]]].index(part)

            def body(o, carry, value=value, part=part, to=held[part], step=step):
                x = value(o)
                holds[part][pl.ds(to + o, step), :] = x
                return fold_max(carry, x)

            best[dest[1]][where] = rows_loop(count, step, body, best[dest[1]][where])
            pending.append((part, held[part], count, dest[1], where, dest[2] * per))
            held[part] += count
    mults = [write_scales(m, b) for m, b in zip(sent, best)]
    for part, at, count, j, where, to in pending:
        base = section_base(outs[j], where) + to
        if count < 16:
            sent[j][base : base + 8, :] = coded(holds[part][at : at + 8, :], mults[j][where])
            sent[j][base + 8 : base + 16, :] = jnp.zeros((8, COLS), S16)
        else:
            encode_rows(holds[part], at, count, sent[j], base, mults[j][where])


def reduce_step(state_parts, groups, keeps, ins, outs, states, msgs):
    parts = tuple(keeps)
    scratch = []
    if outs:
        for p in parts:
            held = sum(g[2] for g in groups if state_parts[g[0]] == p and g[4][0] == "send")
            scratch.append(pltpu.VMEM((held * PER[p], COLS), F32))
    out_shape = [jax.ShapeDtypeStruct((n * PER[p], COLS), F32) for p, n in keeps.items()]
    out_shape += [message(o) for o in outs]
    step = pl.pallas_call(
        functools.partial(step_kernel, state_parts, parts, groups, ins, outs),
        out_shape=out_shape,
        in_specs=[VM] * (len(states) + len(msgs)),
        out_specs=[VM] * len(out_shape),
        scratch_shapes=scratch,
        compiler_params=pltpu.CompilerParams(vmem_limit_bytes=16 * MIB),
        cost_estimate=pl.CostEstimate(flops=int(1e9), transcendentals=0, bytes_accessed=0),
    )
    got = step(*states, *msgs)
    return got[: len(parts)], got[len(parts) :]


def halves(index, start, n, source, at, keep, message_index):
    return (
        (index, start, n, ((source, at),), ("keep", keep)),
        (index, start + n, n, ((source, at + n),), ("send", message_index, 0)),
    )


def sections(n):
    return ((0, n), (1, n))


def reduced(both_d, msg_d, both_e, msg_e):
    whole_d, whole_e = ((0, 128),), ((1, 128),)
    got_d = sends([msg_d], [other_core])
    got_e = sends([msg_e], [other_core])
    dec_a, msgs_a = reduce_step(
        (0,), halves(0, 0, 48, 0, 0, 0, 0), {0: 48},
        (whole_d,), (((0, 48),),), [both_d], got_d,
    )
    got_a = sends(msgs_a, [first_axis(1)])
    state_b, msgs_b = reduce_step(
        (0, 1), halves(0, 96, 16, 0, 96, 0, 0) + halves(1, 0, 64, 1, 0, 0, 0),
        {0: 16, 1: 64}, (whole_d, whole_e), (((0, 16), (1, 64)),), [both_d, both_e], got_d + got_e,
    )
    got_b = sends(msgs_b, [first_axis(3)])
    dec_a, msgs_a = reduce_step(
        (0,), halves(0, 0, 24, 0, 0, 0, 0), {0: 24},
        (((0, 48),),), (((0, 24),),), dec_a, got_a,
    )
    got_a = sends(msgs_a, [first_axis(3)])
    state_b, msgs_b = reduce_step(
        (0, 1), halves(0, 0, 8, 0, 0, 0, 0) + halves(1, 0, 32, 0, 0, 0, 0),
        {0: 8, 1: 32}, (((0, 16), (1, 64)),), (((0, 8), (1, 32)),), state_b, got_b,
    )
    got_b = sends(msgs_b, [first_axis(1)])
    groups = ()
    for b in range(4):
        for index, n, source, to in ((0, 6, 0, 0), (1, 2, 1, 6), (2, 8, 1, 0)):
            dest = ("keep", to) if b == 0 else ("send", b - 1, to)
            groups += ((index, b * n, n, ((source, b * n),), dest),)
    both = (0, 1)
    states, msgs = reduce_step(
        (0, 0, 1), groups, {0: 8, 1: 8},
        (((0, 24),), ((0, 8), (1, 32))), (sections(8),) * 3, dec_a + state_b, got_a + got_b,
    )
    got = sends(msgs, [second_axis(k) for k in (1, 2, 3)])
    groups = ()
    for p in both:
        groups += ((p, 0, 4, tuple((k, 0) for k in range(3)), ("keep", 0)),)
        groups += ((p, 4, 4, tuple((k, 4) for k in range(3)), ("send", 0, 0)),)
    states, msgs = reduce_step(
        both, groups, {0: 4, 1: 4}, (sections(8),) * 3, (sections(4),), states, got
    )
    for i, n in ((0, 2), (1, 1)):
        got = sends(msgs, [z_axis(Z_SHIFTS[i])])
        states, msgs = reduce_step(
            both, halves(0, 0, n, 0, 0, 0, 0) + halves(1, 0, n, 0, 0, 0, 0),
            {0: n, 1: n}, (sections(2 * n),), (sections(n),), states, got,
        )
    got = sends(msgs, [z_axis(Z_SHIFTS[2])])
    groups = tuple((p, 0, 1, ((0, 0),), ("keep", 0)) for p in both)
    states, _ = reduce_step(both, groups, {0: 1, 1: 1}, (sections(1),), (), states, got)
    return states[1], states[0]


def by_size(total, body):
    low = 0
    for rows, depth in SIZES:

        @pl.when((total > low) & (total <= rows))
        def _(rows=rows, depth=depth):
            body(rows, depth)

        low = rows


def second_rows(rows, r0, width):
    row = lax.broadcasted_iota(jnp.int32, (rows, width), 0)
    return ((row < EXTRA) & (row % 2 == 1)) | (row >= EXTRA + r0)


def spread(second, v0, v1):
    return jnp.where(second, jnp.broadcast_to(v1, second.shape), jnp.broadcast_to(v0, second.shape))


def transposed(src, dst, width, depth):
    for k in range(0, depth, 128):
        for n in range(0, width, 512):
            dst[n : n + 512, k : k + 128] = src[k : k + 128, n : n + 512].T


def products(per, lhs_t, rhs, depth, width, hidden, table, base, both, best):
    def column_block(xb, carry):
        b = rhs[0:depth, pl.ds(pl.multiple_of(xb * COLS, COLS), COLS)]
        for n in range(0, width, 256):
            g = dot(lhs_t[n : n + 256, 0:depth], b)
            carry = fold_max(carry, g)
            for r in range(0, 256, per):
                to = table[base + xb * 64 + (n + r) // per]
                both[pl.ds(pl.multiple_of(to * per, per), per), :] = g[r : r + per]
        return carry

    best[...] = lax.fori_loop(0, hidden // COLS, column_block, jnp.zeros((8, COLS), F32))


def encode_other(both, best, msg):
    half = both.shape[0] // 2
    (mult,) = write_scales(msg, [best[...]])
    encode_rows(both, half, half, msg, 0, mult)


def decoder_kernel(
    factor, table, x_hbm, y_hbm, dirs, targets, enc, dec,
    both, msg, jac, along, cols, hid, dec_v,
    x_ref, y_ref, enc_v, dirs_v, targets_v, tgt, pushed, jac_t, best, sems,
):
    _, hidden = enc.shape
    out_width = dec.shape[0]
    rmax = dirs.shape[1]
    wide, high = hidden // 2, out_width // 2
    pairs = [(dirs, dirs_v), (x_hbm, x_ref)]
    pairs += [(enc.at[:, pl.ds(k, wide)], enc_v.at[:, pl.ds(k, wide)]) for k in (0, wide)]
    pairs += [(dec.at[pl.ds(0, high)], dec_v.at[pl.ds(0, high)]), (targets, targets_v)]
    pairs += [(y_hbm, y_ref), (dec.at[pl.ds(high, high)], dec_v.at[pl.ds(high, high)])]
    copies = [pltpu.make_async_copy(a, b, sems.at[i]) for i, (a, b) in enumerate(pairs)]
    for c in copies:
        c.start()
    r0, r1 = table[RANKS_AT], table[RANKS_AT + 1]
    at1 = pl.multiple_of(EXTRA + r0, BLK)
    tail = pl.multiple_of(EXTRA + rmax + r0, BLK)
    for ref in (cols, tgt):
        ref[pl.ds(tail, 256), :] = jnp.zeros((256, ref.shape[1]), BF16)

    def pair(ref):
        v = ref[...].astype(F32)
        odd = lax.broadcasted_iota(jnp.int32, (EXTRA, v.shape[1]), 0) % 2 == 1
        return spread(odd, v[0:1], v[1:2]).astype(BF16)

    copies[0].wait()
    cols[EXTRA : EXTRA + rmax, :] = dirs_v[0]
    cols[pl.ds(at1, rmax), :] = dirs_v[1]
    copies[1].wait()
    cols[0:EXTRA, :] = pair(x_ref)

    def forward(rows, depth):
        second = second_rows(rows, r0, COLS)
        first_row = lax.broadcasted_iota(jnp.int32, (rows, COLS), 0)
        if depth > rows:
            for ref in (pushed, jac):
                ref[rows:depth, :] = jnp.zeros((depth - rows, ref.shape[1]), BF16)

        for n in range(0, hidden, COLS):
            if n % wide == 0:
                copies[2 + n // wide].wait()
            at = slice(n, n + COLS)
            al = dot(cols[0:rows, :], enc_v[:, at])
            along[0:rows, at] = al
            h = jnp.tanh(al[0:EXTRA])
            hid[:, at] = h
            s = 1.0 - h * h
            sl = spread(second, s[0:1], s[1:2])
            pushed[0:rows, at] = (al * sl).astype(BF16)
            pushed[0:EXTRA, at] = h.astype(BF16)
        copies[5].wait()
        tgt[EXTRA : EXTRA + rmax, :] = targets_v[0]
        tgt[pl.ds(at1, rmax), :] = targets_v[1]
        copies[6].wait()
        tgt[0:EXTRA, :] = pair(y_ref)

        def weight_of(rank):
            return (factor * BLK) / jnp.full((rows, COLS), rank, jnp.int32).astype(F32)

        w = jnp.where(first_row >= EXTRA + r0, weight_of(r1), weight_of(r0))
        w = jnp.where(first_row < EXTRA, jnp.where(first_row < 2, factor, 0.0), w)
        w = jnp.where(first_row < EXTRA + r0 + r1, w, 0.0)

        for n in range(0, out_width, high):
            copies[4 if n == 0 else 7].wait()
            at = slice(n, n + high)
            im = dot(pushed[0:rows, :], dec_v[at, :], NT)
            jac[0:rows, at] = ((im - tgt[0:rows, at].astype(F32)) * w).astype(BF16)
        transposed(jac, jac_t, out_width, depth)
        products(PER[0], jac_t, pushed, depth, out_width, hidden, table, 0, both, best)

    by_size(EXTRA + r0 + r1, forward)
    encode_other(both, best, msg)


def encoder_kernel(
    table, jac, along, cols, hid, dec, both, msg, lifted, cols_t, best
):
    in_width = cols.shape[1]
    hidden = dec.shape[1]
    r0, r1 = table[RANKS_AT], table[RANKS_AT + 1]

    def backward(rows, depth):
        second = second_rows(rows, r0, COLS)
        extra_row = lax.broadcasted_iota(jnp.int32, (EXTRA, COLS), 0)
        if depth > rows:
            lifted[rows:depth, :] = jnp.zeros((depth - rows, hidden), BF16)

        def hidden_block(n, carry):
            at = pl.ds(pl.multiple_of(n * COLS, COLS), COLS)
            back = dot(jac[0:rows, :], dec[:, at])
            h = hid[:, at]
            s = 1.0 - h * h
            sl = spread(second, s[0:1], s[1:2])
            up = back * sl
            lifted[0:rows, at] = up.astype(BF16)
            prod = back[EXTRA:] * along[EXTRA:rows, at]
            sec = second[EXTRA:]
            sum0 = jnp.sum(jnp.where(sec, 0.0, prod), axis=0, keepdims=True)
            sum1 = jnp.sum(jnp.where(sec, prod, 0.0), axis=0, keepdims=True)
            sc = -2.0 * h * s * spread(second[0:EXTRA], sum0, sum1)
            hi = sc.astype(BF16).astype(F32)
            mid = (sc - hi).astype(BF16).astype(F32)
            low = sc - hi - mid
            ent = up[0:EXTRA].astype(BF16).astype(F32)
            rest = jnp.where(extra_row < 6, mid, jnp.where(extra_row < 8, low, 0.0))
            fixed = jnp.where(extra_row < 2, ent, jnp.where(extra_row < 4, hi, rest))
            lifted[0:EXTRA, at] = fixed.astype(BF16)
            return carry

        lax.fori_loop(0, hidden // COLS, hidden_block, 0)
        transposed(cols, cols_t, in_width, depth)
        products(PER[1], cols_t, lifted, depth, in_width, hidden, table, 256, both, best)

    by_size(EXTRA + r0 + r1, backward)
    encode_other(both, best, msg)


def own_terms(factor, table, x, y, dirs, targets, enc, dec):
    in_width, hidden = enc.shape
    out_width = dec.shape[0]
    top, depth = SIZES[-1]
    blocks = 128
    shape = jax.ShapeDtypeStruct
    both, msg, jac, along, cols, hid, dec_v = pl.pallas_call(
        functools.partial(decoder_kernel, factor),
        out_shape=[
            shape((2 * blocks * PER[0], COLS), F32),
            message(((0, blocks),)),
            shape((ROWS, out_width), BF16),
            shape((top, hidden), F32),
            shape((ROWS, in_width), BF16),
            shape((EXTRA, hidden), F32),
            shape(dec.shape, BF16),
        ],
        in_specs=[SM] + [HB] * 6,
        out_specs=[VM] * 7,
        scratch_shapes=[
            pltpu.VMEM(x.shape, BF16),
            pltpu.VMEM(y.shape, BF16),
            pltpu.VMEM(enc.shape, BF16),
            pltpu.VMEM(dirs.shape, BF16),
            pltpu.VMEM(targets.shape, BF16),
            pltpu.VMEM((ROWS, out_width), BF16),
            pltpu.VMEM((ROWS, hidden), BF16),
            pltpu.VMEM((out_width, depth), BF16),
            pltpu.VMEM((8, COLS), F32),
            pltpu.SemaphoreType.DMA((8,)),
        ],
        compiler_params=pltpu.CompilerParams(vmem_limit_bytes=18 * MIB),
        cost_estimate=pl.CostEstimate(flops=int(8e9), transcendentals=0, bytes_accessed=0),
        name="decoder_terms",
    )(table, *[pltpu.with_memory_space_constraint(a, pltpu.HBM) for a in (x, y, dirs, targets, enc, dec)])
    encoder_part = pl.pallas_call(
        encoder_kernel,
        out_shape=[
            shape((2 * blocks * PER[1], COLS), F32),
            message(((1, blocks),)),
        ],
        in_specs=[SM] + [VM] * 5,
        out_specs=[VM] * 2,
        scratch_shapes=[
            pltpu.VMEM((ROWS, hidden), BF16),
            pltpu.VMEM((in_width, depth), BF16),
            pltpu.VMEM((8, COLS), F32),
        ],
        compiler_params=pltpu.CompilerParams(vmem_limit_bytes=10 * MIB),
        cost_estimate=pl.CostEstimate(flops=int(6e9), transcendentals=0, bytes_accessed=0),
        name="encoder_terms",
    )
    both_e, msg_e = encoder_part(table, jac, along, cols, hid, dec_v)
    return both, msg, both_e, msg_e


Z_SHIFTS = (1, -1, 3)


def z_partner(shift, z, c):
    return (z + shift) % 8 if z % 2 == c else (z - shift) % 8


def z_place(z, zb, cb):
    place = jnp.zeros_like(zb)
    for code in range(8):
        at, odd = z, (z & 1) ^ cb
        for bit, shift in zip((4, 2, 1), Z_SHIFTS):
            if code & bit:
                at, odd = (at + jnp.where(odd == 0, shift, -shift)) & 7, 1 - odd
        place = place + jnp.where(at == zb, code, 0)
    return place


def place_table(z, y, core, x, ranks):
    i = jnp.arange(640, dtype=jnp.int32)
    xb, zb, yb, cb = (i >> 6) & 3, (i >> 3) & 7, (i >> 1) & 3, i & 1
    encoder = i >= 256
    zp = z_place(z, zb, cb)
    lane_b = encoder | (zp >= 6)
    first = cb == 0
    ea = jnp.where(first, xb ^ x, yb ^ y)
    eb = jnp.where(first, yb - y, xb - x) & 3
    ap = jnp.where(ea == 0, 0, jnp.where(ea == 2, 3, jnp.where((ea == 1) == lane_b, 1, 2)))
    rest = jnp.where(lane_b, 96 + ap * 8 + eb * 2 + zp - 6, ap * 24 + eb * 6 + zp)
    place = jnp.where(cb == core, 0, 128) + jnp.where(encoder, ap * 32 + eb * 8 + zp, rest)
    return jnp.where(i < RANKS_AT, place, 0) + jnp.pad(ranks, (RANKS_AT, 126))


def send(value, fn):
    pairs = []
    for z in range(8):
        for y in range(4):
            for c in range(2):
                for x in range(4):
                    z2, y2, c2, x2 = fn(z, y, c, x)
                    pairs.append((((z * 4 + y) * 2 + c) * 4 + x, ((z2 * 4 + y2) * 2 + c2) * 4 + x2))
    return lax.ppermute(value, ("dp", "mp"), pairs)


def sends(values, ways):
    got = []
    for v, way in zip(values, ways):
        got.append(send(v, way))
    return got


def other_core(z, y, c, x):
    return (z, y, 1 - c, x)


def first_axis(flip):
    return lambda z, y, c, x: (z, y, c, x ^ flip) if c == 0 else (z, y ^ flip, c, x)


def second_axis(k):
    return lambda z, y, c, x: (z, (y + k) % 4, c, x) if c == 0 else (z, y, c, (x + k) % 4)


def z_axis(shift):
    return lambda z, y, c, x: (z_partner(shift, z, c), y, c, x)


def per_device(sample_inputs, sample_outputs, directions, targets, ranks, enc, dec):
    population = sample_inputs.shape[0] * lax.axis_size("dp") * lax.axis_size("mp")
    factor = 2.0 / math.sqrt(population)
    dp = lax.axis_index("dp")
    x = lax.axis_index("mp")
    z, y, core = dp // 8, (dp // 2) % 4, dp % 2
    table = place_table(z, y, core, x, ranks)
    both_d, msg_d, both_e, msg_e = own_terms(
        factor, table, sample_inputs, sample_outputs, directions, targets, enc, dec
    )
    return reduced(both_d, msg_d, both_e, msg_e)


def solution(mesh):
    both = ("dp", "mp")
    in_specs = (
        P(both, None),
        P(both, None),
        P(both, None, None),
        P(both, None, None),
        P(both),
        P(),
        P(),
    )

    return jax.shard_map(
        per_device,
        mesh=mesh,
        in_specs=in_specs,
        out_specs=(P("dp", "mp"), P("dp", "mp")),
        check_vma=False,
    )
```

profile of v0, /device:TPU:8, one launch (start us, length us, event | category | flops | bytes accessed | tf_op | source)
XLA Modules:
  0.0 75.6 jit_solution(16576626076131964720)
XLA Ops:
  0.7 0.7 pad_add_fusion.table
  1.4 7.4 %decoder_terms.1 = (f32[4096,512]{1,0:T(8,128)S(1)}, s16[2064,512]{1,0:T(8,128)(2,1)S(1)}, bf16[784,1024]{1,0:T(8,128)(2,1)S(1)}, f32[528,2048]{1,0:T(8,128)S(1)...) custom-call(s32[640]{0:T(1024)S(1)} %pad_add_fusion.table, ...), custom_call_target="tpu_custom_call" | custom-call | flops 8000000000 | tf_op jit(solution)/shard_map/decoder_terms/pallas_call | solution.py:419
  8.7 0.1 collective-permute-start
  8.8 4.6 %encoder_terms.1 = (f32[2048,512]{1,0:T(8,128)S(1)}, s16[1040,512]{1,0:T(8,128)(2,1)S(1)}) custom-call(s32[640]{0:T(1024)S(1)} %pad_add_fusion.table, bf16[784,1024]{1,0:T(8,128)(2,1)S(1)} %get-tuple-element.42.jac, f32[528,2048]{1,0:T(8,128)S(1)} %get-tuple-element.43.along, bf16[784,512]{1,0:T(8,128)(2,1)S(1)} %get-tuple-element.44.cols, ...), custom_call_target="tpu_custom_call" | custom-call | flops 6000000000 | tf_op jit(solution)/shard_map/encoder_terms/pallas_call | solution.py:465
  13.4 0.6 collective-permute-start.2
  14.0 2.3 %collective-permute-done.2.refs_3_ = s16[1040,512]{1,0:T(8,128)(2,1)S(1)} collective-permute-done((s16[1040,512]{1,0:T(8,128)(2,1)S(1)}, s16[1040,512]{1,0:T(8,128)(2,1)S(1)}, u32[]{:S(2)}, u32[]{:S(2)}) %collective-permute-start.2) | collective-permute-done | bytes 1064992 | tf_op jit(solution)/shard_map/ppermute | solution.py:510
  16.3 0.0 collective-permute-done.refs_1_.refs_2_
  16.3 1.0 %shard_map.88 = (f32[256,512]{1,0:T(8,128)S(1)}, f32[512,512]{1,0:T(8,128)S(1)}, s16[784,512]{1,0:T(8,128)(2,1)S(1)}) custom-call(f32[4096,512]{1,0:T(8,128)S(1)} %get-tuple-element.37.refs_0_, f32[2048,512]{1,0:T(8,128)S(1)} %get-tuple-element.47.refs_1_, s16[2064,512]{1,0:T(8,128)(2,1)S(1)} %collective-permute-done.refs_1_.refs_2_, ...), custom_call_target="tpu_custom_call" | custom-call | flops 1000000000 | tf_op jit(solution)/shard_map/pallas_call | solution.py:178
  17.3 2.8 %collective-permute-start.3 = (s16[784,512]{1,0:T(8,128)(2,1)S(1)}, s16[784,512]{1,0:T(8,128)(2,1)S(1)}, u32[]{:S(2)}, u32[]{:S(2)}) collective-permute-start(s16[784,512]{1,0:T(8,128)(2,1)S(1)} %get-tuple-element.51), channel_id=1, source_target_pairs={{0,3},{1,2},{2,1},{3,0},{4,28},{5,29},{6,30},{7,31},{8,11},{9,10},... | collective-permute-start | bytes 2408456 | tf_op jit(solution)/shard_map/ppermute | solution.py:510
  20.1 1.0 %shard_map.86 = (f32[768,512]{1,0:T(8,128)S(1)}, s16[784,512]{1,0:T(8,128)(2,1)S(1)}) custom-call(f32[4096,512]{1,0:T(8,128)S(1)} %get-tuple-element.37.refs_0_, s16[2064,512]{1,0:T(8,128)(2,1)S(1)} %collective-permute-done.refs_1_.refs_2_), custom_call_target="tpu_custom_call" | custom-call | flops 1000000000 | tf_op jit(solution)/shard_map/pallas_call | solution.py:178
  21.1 0.3 collective-permute-start.1
  21.4 9.3 %collective-permute-done.3.refs_2_ = s16[784,512]{1,0:T(8,128)(2,1)S(1)} collective-permute-done((s16[784,512]{1,0:T(8,128)(2,1)S(1)}, s16[784,512]{1,0:T(8,128)(2,1)S(1)}, u32[]{:S(2)}, u32[]{:S(2)}) %collective-permute-start.3) | collective-permute-done | bytes 802848 | tf_op jit(solution)/shard_map/ppermute | solution.py:510
  30.8 0.5 shard_map.89
  31.3 0.4 collective-permute-start.5
  31.7 1.7 %collective-permute-done.1.refs_1_ = s16[784,512]{1,0:T(8,128)(2,1)S(1)} collective-permute-done((s16[784,512]{1,0:T(8,128)(2,1)S(1)}, s16[784,512]{1,0:T(8,128)(2,1)S(1)}, u32[]{:S(2)}, u32[]{:S(2)}) %collective-permute-start.1) | collective-permute-done | bytes 802848 | tf_op jit(solution)/shard_map/ppermute | solution.py:510
  33.4 0.5 shard_map.87
  33.9 0.9 %collective-permute-start.4 = (s16[400,512]{1,0:T(8,128)(2,1)S(1)}, s16[400,512]{1,0:T(8,128)(2,1)S(1)}, u32[]{:S(2)}, u32[]{:S(2)}) collective-permute-start(s16[400,512]{1,0:T(8,128)(2,1)S(1)} %get-tuple-element.54), channel_id=1, source_target_pairs={{0,3},{1,2},{2,1},{3,0},{4,28},{5,29},{6,30},{7,31},{8,11},{9,10},... | collective-permute-start | bytes 1228808 | tf_op jit(solution)/shard_map/ppermute | solution.py:510
  34.7 4.6 %collective-permute-done.5.refs_4_ = s16[400,512]{1,0:T(8,128)(2,1)S(1)} collective-permute-done((s16[400,512]{1,0:T(8,128)(2,1)S(1)}, s16[400,512]{1,0:T(8,128)(2,1)S(1)}, u32[]{:S(2)}, u32[]{:S(2)}) %collective-permute-start.5) | collective-permute-done | bytes 409632 | tf_op jit(solution)/shard_map/ppermute | solution.py:510
  39.3 3.8 %collective-permute-done.4.refs_3_ = s16[400,512]{1,0:T(8,128)(2,1)S(1)} collective-permute-done((s16[400,512]{1,0:T(8,128)(2,1)S(1)}, s16[400,512]{1,0:T(8,128)(2,1)S(1)}, u32[]{:S(2)}, u32[]{:S(2)}) %collective-permute-start.4) | collective-permute-done | bytes 409632 | tf_op jit(solution)/shard_map/ppermute | solution.py:510
  43.1 0.6 shard_map.90
  43.7 1.7 %collective-permute-start.6 = (s16[208,512]{1,0:T(8,128)(2,1)S(1)}, s16[208,512]{1,0:T(8,128)(2,1)S(1)}, u32[]{:S(2)}, u32[]{:S(2)}) collective-permute-start(s16[208,512]{1,0:T(8,128)(2,1)S(1)} %get-tuple-element.58), channel_id=1, source_target_pairs={{0,8},{1,9},{2,10},{3,11},{4,5},{5,6},{6,7},{7,4},{8,16},{9,17},{1... | collective-permute-start | bytes 638984 | tf_op jit(solution)/shard_map/ppermute | solution.py:510
  45.4 1.0 %collective-permute-start.7 = (s16[208,512]{1,0:T(8,128)(2,1)S(1)}, s16[208,512]{1,0:T(8,128)(2,1)S(1)}, u32[]{:S(2)}, u32[]{:S(2)}) collective-permute-start(s16[208,512]{1,0:T(8,128)(2,1)S(1)} %get-tuple-element.59), channel_id=1, source_target_pairs={{0,16},{1,17},{2,18},{3,19},{4,6},{5,7},{6,4},{7,5},{8,24},{9,25},... | collective-permute-start | bytes 638984 | tf_op jit(solution)/shard_map/ppermute | solution.py:510
  46.3 2.4 %collective-permute-start.8 = (s16[208,512]{1,0:T(8,128)(2,1)S(1)}, s16[208,512]{1,0:T(8,128)(2,1)S(1)}, u32[]{:S(2)}, u32[]{:S(2)}) collective-permute-start(s16[208,512]{1,0:T(8,128)(2,1)S(1)} %get-tuple-element.60), channel_id=1, source_target_pairs={{0,24},{1,25},{2,26},{3,27},{4,7},{5,4},{6,5},{7,6},{8,0},{9,1},{1... | collective-permute-start | bytes 638984 | tf_op jit(solution)/shard_map/ppermute | solution.py:510
  48.7 0.9 %collective-permute-done.6.refs_2_ = s16[208,512]{1,0:T(8,128)(2,1)S(1)} collective-permute-done((s16[208,512]{1,0:T(8,128)(2,1)S(1)}, s16[208,512]{1,0:T(8,128)(2,1)S(1)}, u32[]{:S(2)}, u32[]{:S(2)}) %collective-permute-start.6) | collective-permute-done | bytes 213024 | tf_op jit(solution)/shard_map/ppermute | solution.py:510
  49.6 3.2 %collective-permute-done.7.refs_3_ = s16[208,512]{1,0:T(8,128)(2,1)S(1)} collective-permute-done((s16[208,512]{1,0:T(8,128)(2,1)S(1)}, s16[208,512]{1,0:T(8,128)(2,1)S(1)}, u32[]{:S(2)}, u32[]{:S(2)}) %collective-permute-start.7) | collective-permute-done | bytes 213024 | tf_op jit(solution)/shard_map/ppermute | solution.py:510
  52.8 1.6 %collective-permute-done.8.refs_4_ = s16[208,512]{1,0:T(8,128)(2,1)S(1)} collective-permute-done((s16[208,512]{1,0:T(8,128)(2,1)S(1)}, s16[208,512]{1,0:T(8,128)(2,1)S(1)}, u32[]{:S(2)}, u32[]{:S(2)}) %collective-permute-start.8) | collective-permute-done | bytes 213024 | tf_op jit(solution)/shard_map/ppermute | solution.py:510
  54.5 0.2 shard_map.91
  54.7 3.0 %collective-permute-start.9 = (s16[112,512]{1,0:T(8,128)(2,1)S(1)}, s16[112,512]{1,0:T(8,128)(2,1)S(1)}, u32[]{:S(2)}, u32[]{:S(2)}) collective-permute-start(s16[112,512]{1,0:T(8,128)(2,1)S(1)} %get-tuple-element.63), channel_id=1, source_target_pairs={{0,32},{1,33},{2,34},{3,35},{4,228},{5,229},{6,230},{7,231},{8,40}... | collective-permute-start | bytes 344072 | tf_op jit(solution)/shard_map/ppermute | solution.py:510
  57.7 3.2 %collective-permute-done.9.refs_2_ = s16[112,512]{1,0:T(8,128)(2,1)S(1)} collective-permute-done((s16[112,512]{1,0:T(8,128)(2,1)S(1)}, s16[112,512]{1,0:T(8,128)(2,1)S(1)}, u32[]{:S(2)}, u32[]{:S(2)}) %collective-permute-start.9) | collective-permute-done | bytes 114720 | tf_op jit(solution)/shard_map/ppermute | solution.py:510
  60.9 0.1 shard_map.92
  61.0 5.2 %collective-permute-start.10 = (s16[64,512]{1,0:T(8,128)(2,1)S(1)}, s16[64,512]{1,0:T(8,128)(2,1)S(1)}, u32[]{:S(2)}, u32[]{:S(2)}) collective-permute-start(s16[64,512]{1,0:T(8,128)(2,1)S(1)} %get-tuple-element.66), channel_id=1, source_target_pairs={{0,224},{1,225},{2,226},{3,227},{4,36},{5,37},{6,38},{7,39},{8,232... | collective-permute-start | bytes 196616 | tf_op jit(solution)/shard_map/ppermute | solution.py:510
  66.2 2.5 %collective-permute-done.10.refs_2_ = s16[64,512]{1,0:T(8,128)(2,1)S(1)} collective-permute-done((s16[64,512]{1,0:T(8,128)(2,1)S(1)}, s16[64,512]{1,0:T(8,128)(2,1)S(1)}, u32[]{:S(2)}, u32[]{:S(2)}) %collective-permute-start.10) | collective-permute-done | bytes 65568 | tf_op jit(solution)/shard_map/ppermute | solution.py:510
  68.7 0.1 shard_map.93
  68.7 1.8 %collective-permute-start.11 = (s16[48,512]{1,0:T(8,128)(2,1)S(1)}, s16[48,512]{1,0:T(8,128)(2,1)S(1)}, u32[]{:S(2)}, u32[]{:S(2)}) collective-permute-start(s16[48,512]{1,0:T(8,128)(2,1)S(1)} %get-tuple-element.69), channel_id=1, source_target_pairs={{0,96},{1,97},{2,98},{3,99},{4,164},{5,165},{6,166},{7,167},{8,104... | collective-permute-start | bytes 147464 | tf_op jit(solution)/shard_map/ppermute | solution.py:510
  70.5 4.5 %collective-permute-done.11.refs_2_ = s16[48,512]{1,0:T(8,128)(2,1)S(1)} collective-permute-done((s16[48,512]{1,0:T(8,128)(2,1)S(1)}, s16[48,512]{1,0:T(8,128)(2,1)S(1)}, u32[]{:S(2)}, u32[]{:S(2)}) %collective-permute-start.11) | collective-permute-done | bytes 49184 | tf_op jit(solution)/shard_map/ppermute | solution.py:510
  75.0 0.6 shard_map.94
Async XLA Ops:
  8.7 7.6 %collective-permute-start = (s16[2064,512]{1,0:T(8,128)(2,1)S(1)}, s16[2064,512]{1,0:T(8,128)(2,1)S(1)}, u32[]{:S(2)}, u32[]{:S(2)}) collective-permute-start(s16[2064,512]{1,0:T(8,128)(2,1)S(1)} %get-tuple-element.38), channel_id=1, source_target_pairs={{0,4},{1,5},{2,6},{3,7},{4,0},{5,1},{6,2},{7,3},{8,12},{9,13},{10,... | collective-permute-start | bytes 6340616 | tf_op jit(solution)/shard_map/ppermute | solution.py:510
  13.4 2.9 %collective-permute-start.2 = (s16[1040,512]{1,0:T(8,128)(2,1)S(1)}, s16[1040,512]{1,0:T(8,128)(2,1)S(1)}, u32[]{:S(2)}, u32[]{:S(2)}) collective-permute-start(s16[1040,512]{1,0:T(8,128)(2,1)S(1)} %get-tuple-element.48), channel_id=1, source_target_pairs={{0,4},{1,5},{2,6},{3,7},{4,0},{5,1},{6,2},{7,3},{8,12},{9,13},{10,... | collective-permute-start | bytes 3194888 | tf_op jit(solution)/shard_map/ppermute | solution.py:510
  17.3 13.5 %collective-permute-start.3 = (s16[784,512]{1,0:T(8,128)(2,1)S(1)}, s16[784,512]{1,0:T(8,128)(2,1)S(1)}, u32[]{:S(2)}, u32[]{:S(2)}) collective-permute-start(s16[784,512]{1,0:T(8,128)(2,1)S(1)} %get-tuple-element.51), channel_id=1, source_target_pairs={{0,3},{1,2},{2,1},{3,0},{4,28},{5,29},{6,30},{7,31},{8,11},{9,10},... | collective-permute-start | bytes 2408456 | tf_op jit(solution)/shard_map/ppermute | solution.py:510
  21.1 12.3 %collective-permute-start.1 = (s16[784,512]{1,0:T(8,128)(2,1)S(1)}, s16[784,512]{1,0:T(8,128)(2,1)S(1)}, u32[]{:S(2)}, u32[]{:S(2)}) collective-permute-start(s16[784,512]{1,0:T(8,128)(2,1)S(1)} %get-tuple-element.40), channel_id=1, source_target_pairs={{0,1},{1,0},{2,3},{3,2},{4,12},{5,13},{6,14},{7,15},{8,9},{9,8},{1... | collective-permute-start | bytes 2408456 | tf_op jit(solution)/shard_map/ppermute | solution.py:510
  31.3 8.0 %collective-permute-start.5 = (s16[400,512]{1,0:T(8,128)(2,1)S(1)}, s16[400,512]{1,0:T(8,128)(2,1)S(1)}, u32[]{:S(2)}, u32[]{:S(2)}) collective-permute-start(s16[400,512]{1,0:T(8,128)(2,1)S(1)} %get-tuple-element.55), channel_id=1, source_target_pairs={{0,1},{1,0},{2,3},{3,2},{4,12},{5,13},{6,14},{7,15},{8,9},{9,8},{1... | collective-permute-start | bytes 1228808 | tf_op jit(solution)/shard_map/ppermute | solution.py:510
  33.9 9.2 %collective-permute-start.4 = (s16[400,512]{1,0:T(8,128)(2,1)S(1)}, s16[400,512]{1,0:T(8,128)(2,1)S(1)}, u32[]{:S(2)}, u32[]{:S(2)}) collective-permute-start(s16[400,512]{1,0:T(8,128)(2,1)S(1)} %get-tuple-element.54), channel_id=1, source_target_pairs={{0,3},{1,2},{2,1},{3,0},{4,28},{5,29},{6,30},{7,31},{8,11},{9,10},... | collective-permute-start | bytes 1228808 | tf_op jit(solution)/shard_map/ppermute | solution.py:510
  43.7 5.9 %collective-permute-start.6 = (s16[208,512]{1,0:T(8,128)(2,1)S(1)}, s16[208,512]{1,0:T(8,128)(2,1)S(1)}, u32[]{:S(2)}, u32[]{:S(2)}) collective-permute-start(s16[208,512]{1,0:T(8,128)(2,1)S(1)} %get-tuple-element.58), channel_id=1, source_target_pairs={{0,8},{1,9},{2,10},{3,11},{4,5},{5,6},{6,7},{7,4},{8,16},{9,17},{1... | collective-permute-start | bytes 638984 | tf_op jit(solution)/shard_map/ppermute | solution.py:510
  45.4 7.5 %collective-permute-start.7 = (s16[208,512]{1,0:T(8,128)(2,1)S(1)}, s16[208,512]{1,0:T(8,128)(2,1)S(1)}, u32[]{:S(2)}, u32[]{:S(2)}) collective-permute-start(s16[208,512]{1,0:T(8,128)(2,1)S(1)} %get-tuple-element.59), channel_id=1, source_target_pairs={{0,16},{1,17},{2,18},{3,19},{4,6},{5,7},{6,4},{7,5},{8,24},{9,25},... | collective-permute-start | bytes 638984 | tf_op jit(solution)/shard_map/ppermute | solution.py:510
  46.3 8.1 %collective-permute-start.8 = (s16[208,512]{1,0:T(8,128)(2,1)S(1)}, s16[208,512]{1,0:T(8,128)(2,1)S(1)}, u32[]{:S(2)}, u32[]{:S(2)}) collective-permute-start(s16[208,512]{1,0:T(8,128)(2,1)S(1)} %get-tuple-element.60), channel_id=1, source_target_pairs={{0,24},{1,25},{2,26},{3,27},{4,7},{5,4},{6,5},{7,6},{8,0},{9,1},{1... | collective-permute-start | bytes 638984 | tf_op jit(solution)/shard_map/ppermute | solution.py:510
  54.7 6.2 %collective-permute-start.9 = (s16[112,512]{1,0:T(8,128)(2,1)S(1)}, s16[112,512]{1,0:T(8,128)(2,1)S(1)}, u32[]{:S(2)}, u32[]{:S(2)}) collective-permute-start(s16[112,512]{1,0:T(8,128)(2,1)S(1)} %get-tuple-element.63), channel_id=1, source_target_pairs={{0,32},{1,33},{2,34},{3,35},{4,228},{5,229},{6,230},{7,231},{8,40}... | collective-permute-start | bytes 344072 | tf_op jit(solution)/shard_map/ppermute | solution.py:510
  61.0 7.7 %collective-permute-start.10 = (s16[64,512]{1,0:T(8,128)(2,1)S(1)}, s16[64,512]{1,0:T(8,128)(2,1)S(1)}, u32[]{:S(2)}, u32[]{:S(2)}) collective-permute-start(s16[64,512]{1,0:T(8,128)(2,1)S(1)} %get-tuple-element.66), channel_id=1, source_target_pairs={{0,224},{1,225},{2,226},{3,227},{4,36},{5,37},{6,38},{7,39},{8,232... | collective-permute-start | bytes 196616 | tf_op jit(solution)/shard_map/ppermute | solution.py:510
  68.7 6.3 %collective-permute-start.11 = (s16[48,512]{1,0:T(8,128)(2,1)S(1)}, s16[48,512]{1,0:T(8,128)(2,1)S(1)}, u32[]{:S(2)}, u32[]{:S(2)}) collective-permute-start(s16[48,512]{1,0:T(8,128)(2,1)S(1)} %get-tuple-element.69), channel_id=1, source_target_pairs={{0,96},{1,97},{2,98},{3,99},{4,164},{5,165},{6,166},{7,167},{8,104... | collective-permute-start | bytes 147464 | tf_op jit(solution)/shard_map/ppermute | solution.py:510
where the time goes:
time: 76.3 us; the launch traced here: 75.6 us
  waiting for transfers between devices  37.6 us (49%)
  starting transfers between devices  20.1 us (26%)
  Pallas kernels  16.5 us (22%)
    ppermute x12, waiting for transfers between devices, send(): return lax.ppermute(value, ('dp', 'mp'), pairs)  37.6 us
    ppermute x12, starting transfers between devices, send(): return lax.ppermute(value, ('dp', 'mp'), pairs)  20.1 us
    pallas_call x1, Pallas kernels, own_terms(): pl.pallas_call(functools.partial(decoder_kernel, factor), out_shape=[shap...  7.36 us
    pallas_call x1, Pallas kernels, own_terms(): both_e, msg_e = encoder_part(table, jac, along, cols, hid, dec_v)  4.57 us
    pallas_call x9, Pallas kernels, reduce_step(): got = step(*states, *msgs)  4.54 us
  transfers between devices with their start and end apart: 12, of which 11 were waited for; matrix products, arithmetic and copies ran while one was open for 0% of the time, Pallas kernels for 9%

commit v1 on v0

--- a/solution.py
+++ b/solution.py
@@ -39,7 +39,7 @@
 
 
 def message(sections):
-    rows = -(-section_base(sections, len(sections)) // 16) * 16 + 16
+    rows = section_base(sections, len(sections)) + 8
     return jax.ShapeDtypeStruct((rows, COLS), S16)
 
 
@@ -69,17 +69,28 @@
     return best
 
 
+def quads(best):
+    top = lax.broadcasted_iota(jnp.int32, (8, COLS), 0) < 4
+    es = [exponents(jnp.maximum(b, pltpu.roll(b, 4, 0))) for b in best]
+    return es, jnp.where(top, es[0], es[-1]).astype(jnp.int32).astype(S16)
+
+
 def write_scales(msg, best):
-    es = [exponents(b) for b in best]
-    last = jnp.concatenate([es[0], es[-1]], axis=0).astype(jnp.int32).astype(S16)
-    msg[msg.shape[0] - 16 :, :] = last
-    return [power(-e) * TOP for e in es]
+    es, rows = quads(best)
+    at = msg.shape[0] - 8
+    if at % 16 == 0:
+        msg[at:, :] = rows
+    return [power(-e) * TOP for e in es], rows
 
 
 def read_scales(msg):
-    e = msg[msg.shape[0] - 16 :, :].astype(jnp.int32).astype(F32)
-    s = power(e) * (1.0 / TOP)
-    return s[0:8], s[8:16]
+    top = lax.broadcasted_iota(jnp.int32, (8, COLS), 0) < 4
+    at = msg.shape[0] - 8
+    tile = msg[at // 16 * 16 :, :].astype(jnp.int32).astype(F32)
+    e = tile[tile.shape[0] - 8 :]
+    other = pltpu.roll(e, 4, 0)
+    scale = 1.0 / TOP
+    return power(jnp.where(top, e, other)) * scale, power(jnp.where(top, other, e)) * scale
 
 
 def rows_loop(count, step, body, init):
@@ -147,14 +158,14 @@
             best[dest[1]][where] = rows_loop(count, step, body, best[dest[1]][where])
             pending.append((part, held[part], count, dest[1], where, dest[2] * per))
             held[part] += count
-    mults = [write_scales(m, b) for m, b in zip(sent, best)]
+    coding = [write_scales(m, b) for m, b in zip(sent, best)]
     for part, at, count, j, where, to in pending:
         base = section_base(outs[j], where) + to
         if count < 16:
-            sent[j][base : base + 8, :] = coded(holds[part][at : at + 8, :], mults[j][where])
-            sent[j][base + 8 : base + 16, :] = jnp.zeros((8, COLS), S16)
+            last = coded(holds[part][at : at + 8, :], coding[j][0][where])
+            sent[j][base : base + 16, :] = jnp.concatenate([last, coding[j][1]], axis=0)
         else:
-            encode_rows(holds[part], at, count, sent[j], base, mults[j][where])
+            encode_rows(holds[part], at, count, sent[j], base, coding[j][0][where])
 
 
 def reduce_step(state_parts, groups, keeps, ins, outs, states, msgs):
@@ -195,34 +206,34 @@
     got_d = sends([msg_d], [other_core])
     got_e = sends([msg_e], [other_core])
     dec_a, msgs_a = reduce_step(
-        (0,), halves(0, 0, 48, 0, 0, 0, 0), {0: 48},
-        (whole_d,), (((0, 48),),), [both_d], got_d,
+        (0,), halves(0, 0, 56, 0, 0, 0, 0), {0: 56},
+        (whole_d,), (((0, 56),),), [both_d], got_d,
     )
     got_a = sends(msgs_a, [first_axis(1)])
     state_b, msgs_b = reduce_step(
-        (0, 1), halves(0, 96, 16, 0, 96, 0, 0) + halves(1, 0, 64, 1, 0, 0, 0),
-        {0: 16, 1: 64}, (whole_d, whole_e), (((0, 16), (1, 64)),), [both_d, both_e], got_d + got_e,
+        (0, 1), halves(0, 112, 8, 0, 112, 0, 0) + halves(1, 0, 64, 1, 0, 0, 0),
+        {0: 8, 1: 64}, (whole_d, whole_e), (((0, 8), (1, 64)),), [both_d, both_e], got_d + got_e,
     )
     got_b = sends(msgs_b, [first_axis(3)])
     dec_a, msgs_a = reduce_step(
-        (0,), halves(0, 0, 24, 0, 0, 0, 0), {0: 24},
-        (((0, 48),),), (((0, 24),),), dec_a, got_a,
+        (0,), halves(0, 0, 28, 0, 0, 0, 0), {0: 28},
+        (((0, 56),),), (((0, 28),),), dec_a, got_a,
     )
     got_a = sends(msgs_a, [first_axis(3)])
     state_b, msgs_b = reduce_step(
-        (0, 1), halves(0, 0, 8, 0, 0, 0, 0) + halves(1, 0, 32, 0, 0, 0, 0),
-        {0: 8, 1: 32}, (((0, 16), (1, 64)),), (((0, 8), (1, 32)),), state_b, got_b,
+        (0, 1), halves(0, 0, 4, 0, 0, 0, 0) + halves(1, 0, 32, 0, 0, 0, 0),
+        {0: 4, 1: 32}, (((0, 8), (1, 64)),), (((0, 4), (1, 32)),), state_b, got_b,
     )
     got_b = sends(msgs_b, [first_axis(1)])
     groups = ()
     for b in range(4):
-        for index, n, source, to in ((0, 6, 0, 0), (1, 2, 1, 6), (2, 8, 1, 0)):
+        for index, n, source, to in ((0, 7, 0, 0), (1, 1, 1, 7), (2, 8, 1, 0)):
             dest = ("keep", to) if b == 0 else ("send", b - 1, to)
             groups += ((index, b * n, n, ((source, b * n),), dest),)
     both = (0, 1)
     states, msgs = reduce_step(
         (0, 0, 1), groups, {0: 8, 1: 8},
-        (((0, 24),), ((0, 8), (1, 32))), (sections(8),) * 3, dec_a + state_b, got_a + got_b,
+        (((0, 28),), ((0, 4), (1, 32))), (sections(8),) * 3, dec_a + state_b, got_a + got_b,
     )
     got = sends(msgs, [second_axis(k) for k in (1, 2, 3)])
     groups = ()
@@ -286,7 +297,7 @@
 
 def encode_other(both, best, msg):
     half = both.shape[0] // 2
-    (mult,) = write_scales(msg, [best[...]])
+    ((mult,), _) = write_scales(msg, [best[...]])
     encode_rows(both, half, half, msg, 0, mult)
 
 
@@ -489,12 +500,12 @@
     xb, zb, yb, cb = (i >> 6) & 3, (i >> 3) & 7, (i >> 1) & 3, i & 1
     encoder = i >= 256
     zp = z_place(z, zb, cb)
-    lane_b = encoder | (zp >= 6)
+    lane_b = encoder | (zp >= 7)
     first = cb == 0
     ea = jnp.where(first, xb ^ x, yb ^ y)
     eb = jnp.where(first, yb - y, xb - x) & 3
     ap = jnp.where(ea == 0, 0, jnp.where(ea == 2, 3, jnp.where((ea == 1) == lane_b, 1, 2)))
-    rest = jnp.where(lane_b, 96 + ap * 8 + eb * 2 + zp - 6, ap * 24 + eb * 6 + zp)
+    rest = jnp.where(lane_b, 112 + ap * 4 + eb, ap * 28 + eb * 7 + zp)
     place = jnp.where(cb == core, 0, 128) + jnp.where(encoder, ap * 32 + eb * 8 + zp, rest)
     return jnp.where(i < RANKS_AT, place, 0) + jnp.pad(ranks, (RANKS_AT, 126))
 

time: 76.3 us -> 72.3 us (0.948)
  waiting for transfers between devices: 37.6 us -> 30.8 us
  starting transfers between devices: 20.1 us -> 22.8 us
    ppermute x12, waiting for transfers between devices: 37.6 us -> 30.8 us  [send(): return lax.ppermute(value, ('dp', 'mp'), pairs)]
    ppermute x12, starting transfers between devices: 20.1 us -> 22.8 us  [send(): return lax.ppermute(value, ('dp', 'mp'), pairs)]
  transfers between devices with their start and end apart: 12 -> 12, of which waited for: 11 -> 8; matrix products, arithmetic and copies ran while one was open for 0% -> 0% of each run, Pallas kernels for 9% -> 11%
where the time goes in v1:
time: 72.3 us; the launch traced here: 71.7 us
  waiting for transfers between devices  30.8 us (43%)
  starting transfers between devices  22.8 us (32%)
  Pallas kernels  16.6 us (23%)
  between operations  0.76 us (1%)
    ppermute x12, waiting for transfers between devices, send(): return lax.ppermute(value, ('dp', 'mp'), pairs)  30.8 us
    ppermute x12, starting transfers between devices, send(): return lax.ppermute(value, ('dp', 'mp'), pairs)  22.8 us
    pallas_call x1, Pallas kernels, own_terms(): pl.pallas_call(functools.partial(decoder_kernel, factor), out_shape=[shap...  7.35 us
    pallas_call x9, Pallas kernels, reduce_step(): got = step(*states, *msgs)  4.74 us
    pallas_call x1, Pallas kernels, own_terms(): both_e, msg_e = encoder_part(table, jac, along, cols, hid, dec_v)  4.56 us
  transfers between devices with their start and end apart: 12, of which 8 were waited for; matrix products, arithmetic and copies ran while one was open for 0% of the time, Pallas kernels for 11%

profile of v1, /device:TPU:8, one launch (start us, length us, event | category | flops | bytes accessed | tf_op | source)
XLA Modules:
  0.0 71.7 jit_solution(4240785721420547421)
XLA Ops:
  0.7 0.7 pad_add_fusion.table
  1.4 7.3 %decoder_terms.1 = (f32[4096,512]{1,0:T(8,128)S(1)}, s16[2056,512]{1,0:T(8,128)(2,1)S(1)}, bf16[784,1024]{1,0:T(8,128)(2,1)S(1)}, f32[528,2048]{1,0:T(8,128)S(1)...) custom-call(s32[640]{0:T(1024)S(1)} %pad_add_fusion.table, ...), custom_call_target="tpu_custom_call" | custom-call | flops 8000000000 | tf_op jit(solution)/shard_map/decoder_terms/pallas_call | solution.py:430
  8.7 0.1 collective-permute-start
  8.8 4.6 %encoder_terms.1 = (f32[2048,512]{1,0:T(8,128)S(1)}, s16[1032,512]{1,0:T(8,128)(2,1)S(1)}) custom-call(s32[640]{0:T(1024)S(1)} %pad_add_fusion.table, bf16[784,1024]{1,0:T(8,128)(2,1)S(1)} %get-tuple-element.42.jac, f32[528,2048]{1,0:T(8,128)S(1)} %get-tuple-element.43.along, bf16[784,512]{1,0:T(8,128)(2,1)S(1)} %get-tuple-element.44.cols, ...), custom_call_target="tpu_custom_call" | custom-call | flops 6000000000 | tf_op jit(solution)/shard_map/encoder_terms/pallas_call | solution.py:476
  13.4 0.6 collective-permute-start.2
  14.0 0.0 collective-permute-done.refs_1_.refs_2_
  14.0 1.1 %shard_map.86 = (f32[896,512]{1,0:T(8,128)S(1)}, s16[904,512]{1,0:T(8,128)(2,1)S(1)}) custom-call(f32[4096,512]{1,0:T(8,128)S(1)} %get-tuple-element.37.refs_0_, s16[2056,512]{1,0:T(8,128)(2,1)S(1)} %collective-permute-done.refs_1_.refs_2_), custom_call_target="tpu_custom_call" | custom-call | flops 1000000000 | tf_op jit(solution)/shard_map/pallas_call | solution.py:189
  15.1 1.6 %collective-permute-start.1 = (s16[904,512]{1,0:T(8,128)(2,1)S(1)}, s16[904,512]{1,0:T(8,128)(2,1)S(1)}, u32[]{:S(2)}, u32[]{:S(2)}) collective-permute-start(s16[904,512]{1,0:T(8,128)(2,1)S(1)} %get-tuple-element.40), channel_id=1, source_target_pairs={{0,1},{1,0},{2,3},{3,2},{4,12},{5,13},{6,14},{7,15},{8,9},{9,8},{1... | collective-permute-start | bytes 2777096 | tf_op jit(solution)/shard_map/ppermute | solution.py:521
  16.7 0.0 collective-permute-done.2.refs_3_
  16.7 0.9 %shard_map.88 = (f32[128,512]{1,0:T(8,128)S(1)}, f32[512,512]{1,0:T(8,128)S(1)}, s16[648,512]{1,0:T(8,128)(2,1)S(1)}) custom-call(f32[4096,512]{1,0:T(8,128)S(1)} %get-tuple-element.37.refs_0_, f32[2048,512]{1,0:T(8,128)S(1)} %get-tuple-element.47.refs_1_, s16[2056,512]{1,0:T(8,128)(2,1)S(1)} %collective-permute-done.refs_1_.refs_2_, ...), custom_call_target="tpu_custom_call" | custom-call | flops 1000000000 | tf_op jit(solution)/shard_map/pallas_call | solution.py:189
  17.6 2.4 %collective-permute-start.3 = (s16[648,512]{1,0:T(8,128)(2,1)S(1)}, s16[648,512]{1,0:T(8,128)(2,1)S(1)}, u32[]{:S(2)}, u32[]{:S(2)}) collective-permute-start(s16[648,512]{1,0:T(8,128)(2,1)S(1)} %get-tuple-element.51), channel_id=1, source_target_pairs={{0,3},{1,2},{2,1},{3,0},{4,28},{5,29},{6,30},{7,31},{8,11},{9,10},... | collective-permute-start | bytes 1990664 | tf_op jit(solution)/shard_map/ppermute | solution.py:521
  20.0 8.7 %collective-permute-done.1.refs_1_ = s16[904,512]{1,0:T(8,128)(2,1)S(1)} collective-permute-done((s16[904,512]{1,0:T(8,128)(2,1)S(1)}, s16[904,512]{1,0:T(8,128)(2,1)S(1)}, u32[]{:S(2)}, u32[]{:S(2)}) %collective-permute-start.1) | collective-permute-done | bytes 925728 | tf_op jit(solution)/shard_map/ppermute | solution.py:521
  28.7 0.6 shard_map.87
  29.3 2.9 %collective-permute-start.4 = (s16[456,512]{1,0:T(8,128)(2,1)S(1)}, s16[456,512]{1,0:T(8,128)(2,1)S(1)}, u32[]{:S(2)}, u32[]{:S(2)}) collective-permute-start(s16[456,512]{1,0:T(8,128)(2,1)S(1)} %get-tuple-element.54), channel_id=1, source_target_pairs={{0,3},{1,2},{2,1},{3,0},{4,28},{5,29},{6,30},{7,31},{8,11},{9,10},... | collective-permute-start | bytes 1400840 | tf_op jit(solution)/shard_map/ppermute | solution.py:521
  32.1 0.0 collective-permute-done.3.refs_2_
  32.1 0.4 shard_map.89
  32.5 0.3 collective-permute-start.5
  32.8 6.9 %collective-permute-done.5.refs_4_ = s16[328,512]{1,0:T(8,128)(2,1)S(1)} collective-permute-done((s16[328,512]{1,0:T(8,128)(2,1)S(1)}, s16[328,512]{1,0:T(8,128)(2,1)S(1)}, u32[]{:S(2)}, u32[]{:S(2)}) %collective-permute-start.5) | collective-permute-done | bytes 335904 | tf_op jit(solution)/shard_map/ppermute | solution.py:521
  39.8 0.0 collective-permute-done.4.refs_3_
  39.8 0.8 %shard_map.90 = (f32[128,512]{1,0:T(8,128)S(1)}, f32[64,512]{1,0:T(8,128)S(1)}, s16[200,512]{1,0:T(8,128)(2,1)S(1)}, s16[200,512]{1,0:T(8,128)(2,1)S(1)}, s16[200,512]{1,0:T(8,128)(2,1)S(1)}) custom-call(f32[448,512]{1,0:T(8,128)S(1)} %get-tuple-element.41.refs_0_, f32[64,512]{1,0:T(8,128)S(1)} %get-tuple-element.52.refs_1_, ...), custom_call_target="tpu_custom_call" | custom-call | flops 1000000000 | tf_op jit(solution)/shard_map/pallas_call | solution.py:189
  40.5 1.7 %collective-permute-start.6 = (s16[200,512]{1,0:T(8,128)(2,1)S(1)}, s16[200,512]{1,0:T(8,128)(2,1)S(1)}, u32[]{:S(2)}, u32[]{:S(2)}) collective-permute-start(s16[200,512]{1,0:T(8,128)(2,1)S(1)} %get-tuple-element.58), channel_id=1, source_target_pairs={{0,8},{1,9},{2,10},{3,11},{4,5},{5,6},{6,7},{7,4},{8,16},{9,17},{1... | collective-permute-start | bytes 614408 | tf_op jit(solution)/shard_map/ppermute | solution.py:521
  42.2 2.0 %collective-permute-start.7 = (s16[200,512]{1,0:T(8,128)(2,1)S(1)}, s16[200,512]{1,0:T(8,128)(2,1)S(1)}, u32[]{:S(2)}, u32[]{:S(2)}) collective-permute-start(s16[200,512]{1,0:T(8,128)(2,1)S(1)} %get-tuple-element.59), channel_id=1, source_target_pairs={{0,16},{1,17},{2,18},{3,19},{4,6},{5,7},{6,4},{7,5},{8,24},{9,25},... | collective-permute-start | bytes 614408 | tf_op jit(solution)/shard_map/ppermute | solution.py:521
  44.2 1.4 %collective-permute-start.8 = (s16[200,512]{1,0:T(8,128)(2,1)S(1)}, s16[200,512]{1,0:T(8,128)(2,1)S(1)}, u32[]{:S(2)}, u32[]{:S(2)}) collective-permute-start(s16[200,512]{1,0:T(8,128)(2,1)S(1)} %get-tuple-element.60), channel_id=1, source_target_pairs={{0,24},{1,25},{2,26},{3,27},{4,7},{5,4},{6,5},{7,6},{8,0},{9,1},{1... | collective-permute-start | bytes 614408 | tf_op jit(solution)/shard_map/ppermute | solution.py:521
  45.5 0.8 %collective-permute-done.6.refs_2_ = s16[200,512]{1,0:T(8,128)(2,1)S(1)} collective-permute-done((s16[200,512]{1,0:T(8,128)(2,1)S(1)}, s16[200,512]{1,0:T(8,128)(2,1)S(1)}, u32[]{:S(2)}, u32[]{:S(2)}) %collective-permute-start.6) | collective-permute-done | bytes 204832 | tf_op jit(solution)/shard_map/ppermute | solution.py:521
  46.4 3.2 %collective-permute-done.7.refs_3_ = s16[200,512]{1,0:T(8,128)(2,1)S(1)} collective-permute-done((s16[200,512]{1,0:T(8,128)(2,1)S(1)}, s16[200,512]{1,0:T(8,128)(2,1)S(1)}, u32[]{:S(2)}, u32[]{:S(2)}) %collective-permute-start.7) | collective-permute-done | bytes 204832 | tf_op jit(solution)/shard_map/ppermute | solution.py:521
  49.6 2.1 %collective-permute-done.8.refs_4_ = s16[200,512]{1,0:T(8,128)(2,1)S(1)} collective-permute-done((s16[200,512]{1,0:T(8,128)(2,1)S(1)}, s16[200,512]{1,0:T(8,128)(2,1)S(1)}, u32[]{:S(2)}, u32[]{:S(2)}) %collective-permute-start.8) | collective-permute-done | bytes 204832 | tf_op jit(solution)/shard_map/ppermute | solution.py:521
  51.7 0.2 shard_map.91
  51.9 2.1 %collective-permute-start.9 = (s16[104,512]{1,0:T(8,128)(2,1)S(1)}, s16[104,512]{1,0:T(8,128)(2,1)S(1)}, u32[]{:S(2)}, u32[]{:S(2)}) collective-permute-start(s16[104,512]{1,0:T(8,128)(2,1)S(1)} %get-tuple-element.63), channel_id=1, source_target_pairs={{0,32},{1,33},{2,34},{3,35},{4,228},{5,229},{6,230},{7,231},{8,40}... | collective-permute-start | bytes 319496 | tf_op jit(solution)/shard_map/ppermute | solution.py:521
  54.0 2.8 %collective-permute-done.9.refs_2_ = s16[104,512]{1,0:T(8,128)(2,1)S(1)} collective-permute-done((s16[104,512]{1,0:T(8,128)(2,1)S(1)}, s16[104,512]{1,0:T(8,128)(2,1)S(1)}, u32[]{:S(2)}, u32[]{:S(2)}) %collective-permute-start.9) | collective-permute-done | bytes 106528 | tf_op jit(solution)/shard_map/ppermute | solution.py:521
  56.8 0.1 shard_map.92
  56.9 5.8 %collective-permute-start.10 = (s16[56,512]{1,0:T(8,128)(2,1)S(1)}, s16[56,512]{1,0:T(8,128)(2,1)S(1)}, u32[]{:S(2)}, u32[]{:S(2)}) collective-permute-start(s16[56,512]{1,0:T(8,128)(2,1)S(1)} %get-tuple-element.66), channel_id=1, source_target_pairs={{0,224},{1,225},{2,226},{3,227},{4,36},{5,37},{6,38},{7,39},{8,232... | collective-permute-start | bytes 172040 | tf_op jit(solution)/shard_map/ppermute | solution.py:521
  62.7 2.2 %collective-permute-done.10.refs_2_ = s16[56,512]{1,0:T(8,128)(2,1)S(1)} collective-permute-done((s16[56,512]{1,0:T(8,128)(2,1)S(1)}, s16[56,512]{1,0:T(8,128)(2,1)S(1)}, u32[]{:S(2)}, u32[]{:S(2)}) %collective-permute-start.10) | collective-permute-done | bytes 57376 | tf_op jit(solution)/shard_map/ppermute | solution.py:521
  64.9 0.1 shard_map.93
  65.0 2.0 %collective-permute-start.11 = (s16[32,512]{1,0:T(8,128)(2,1)S(1)}, s16[32,512]{1,0:T(8,128)(2,1)S(1)}, u32[]{:S(2)}, u32[]{:S(2)}) collective-permute-start(s16[32,512]{1,0:T(8,128)(2,1)S(1)} %get-tuple-element.69), channel_id=1, source_target_pairs={{0,96},{1,97},{2,98},{3,99},{4,164},{5,165},{6,166},{7,167},{8,104... | collective-permute-start | bytes 98312 | tf_op jit(solution)/shard_map/ppermute | solution.py:521
  67.0 4.1 %collective-permute-done.11.refs_2_ = s16[32,512]{1,0:T(8,128)(2,1)S(1)} collective-permute-done((s16[32,512]{1,0:T(8,128)(2,1)S(1)}, s16[32,512]{1,0:T(8,128)(2,1)S(1)}, u32[]{:S(2)}, u32[]{:S(2)}) %collective-permute-start.11) | collective-permute-done | bytes 32800 | tf_op jit(solution)/shard_map/ppermute | solution.py:521
  71.1 0.6 shard_map.94
Async XLA Ops:
  8.7 5.3 %collective-permute-start = (s16[2056,512]{1,0:T(8,128)(2,1)S(1)}, s16[2056,512]{1,0:T(8,128)(2,1)S(1)}, u32[]{:S(2)}, u32[]{:S(2)}) collective-permute-start(s16[2056,512]{1,0:T(8,128)(2,1)S(1)} %get-tuple-element.38), channel_id=1, source_target_pairs={{0,4},{1,5},{2,6},{3,7},{4,0},{5,1},{6,2},{7,3},{8,12},{9,13},{10,... | collective-permute-start | bytes 6316040 | tf_op jit(solution)/shard_map/ppermute | solution.py:521
  13.4 3.3 %collective-permute-start.2 = (s16[1032,512]{1,0:T(8,128)(2,1)S(1)}, s16[1032,512]{1,0:T(8,128)(2,1)S(1)}, u32[]{:S(2)}, u32[]{:S(2)}) collective-permute-start(s16[1032,512]{1,0:T(8,128)(2,1)S(1)} %get-tuple-element.48), channel_id=1, source_target_pairs={{0,4},{1,5},{2,6},{3,7},{4,0},{5,1},{6,2},{7,3},{8,12},{9,13},{10,... | collective-permute-start | bytes 3170312 | tf_op jit(solution)/shard_map/ppermute | solution.py:521
  15.1 13.6 %collective-permute-start.1 = (s16[904,512]{1,0:T(8,128)(2,1)S(1)}, s16[904,512]{1,0:T(8,128)(2,1)S(1)}, u32[]{:S(2)}, u32[]{:S(2)}) collective-permute-start(s16[904,512]{1,0:T(8,128)(2,1)S(1)} %get-tuple-element.40), channel_id=1, source_target_pairs={{0,1},{1,0},{2,3},{3,2},{4,12},{5,13},{6,14},{7,15},{8,9},{9,8},{1... | collective-permute-start | bytes 2777096 | tf_op jit(solution)/shard_map/ppermute | solution.py:521
  17.6 14.5 %collective-permute-start.3 = (s16[648,512]{1,0:T(8,128)(2,1)S(1)}, s16[648,512]{1,0:T(8,128)(2,1)S(1)}, u32[]{:S(2)}, u32[]{:S(2)}) collective-permute-start(s16[648,512]{1,0:T(8,128)(2,1)S(1)} %get-tuple-element.51), channel_id=1, source_target_pairs={{0,3},{1,2},{2,1},{3,0},{4,28},{5,29},{6,30},{7,31},{8,11},{9,10},... | collective-permute-start | bytes 1990664 | tf_op jit(solution)/shard_map/ppermute | solution.py:521
  29.3 10.5 %collective-permute-start.4 = (s16[456,512]{1,0:T(8,128)(2,1)S(1)}, s16[456,512]{1,0:T(8,128)(2,1)S(1)}, u32[]{:S(2)}, u32[]{:S(2)}) collective-permute-start(s16[456,512]{1,0:T(8,128)(2,1)S(1)} %get-tuple-element.54), channel_id=1, source_target_pairs={{0,3},{1,2},{2,1},{3,0},{4,28},{5,29},{6,30},{7,31},{8,11},{9,10},... | collective-permute-start | bytes 1400840 | tf_op jit(solution)/shard_map/ppermute | solution.py:521
  32.5 7.2 %collective-permute-start.5 = (s16[328,512]{1,0:T(8,128)(2,1)S(1)}, s16[328,512]{1,0:T(8,128)(2,1)S(1)}, u32[]{:S(2)}, u32[]{:S(2)}) collective-permute-start(s16[328,512]{1,0:T(8,128)(2,1)S(1)} %get-tuple-element.55), channel_id=1, source_target_pairs={{0,1},{1,0},{2,3},{3,2},{4,12},{5,13},{6,14},{7,15},{8,9},{9,8},{1... | collective-permute-start | bytes 1007624 | tf_op jit(solution)/shard_map/ppermute | solution.py:521
  40.5 5.8 %collective-permute-start.6 = (s16[200,512]{1,0:T(8,128)(2,1)S(1)}, s16[200,512]{1,0:T(8,128)(2,1)S(1)}, u32[]{:S(2)}, u32[]{:S(2)}) collective-permute-start(s16[200,512]{1,0:T(8,128)(2,1)S(1)} %get-tuple-element.58), channel_id=1, source_target_pairs={{0,8},{1,9},{2,10},{3,11},{4,5},{5,6},{6,7},{7,4},{8,16},{9,17},{1... | collective-permute-start | bytes 614408 | tf_op jit(solution)/shard_map/ppermute | solution.py:521
  42.2 7.4 %collective-permute-start.7 = (s16[200,512]{1,0:T(8,128)(2,1)S(1)}, s16[200,512]{1,0:T(8,128)(2,1)S(1)}, u32[]{:S(2)}, u32[]{:S(2)}) collective-permute-start(s16[200,512]{1,0:T(8,128)(2,1)S(1)} %get-tuple-element.59), channel_id=1, source_target_pairs={{0,16},{1,17},{2,18},{3,19},{4,6},{5,7},{6,4},{7,5},{8,24},{9,25},... | collective-permute-start | bytes 614408 | tf_op jit(solution)/shard_map/ppermute | solution.py:521
  44.2 7.5 %collective-permute-start.8 = (s16[200,512]{1,0:T(8,128)(2,1)S(1)}, s16[200,512]{1,0:T(8,128)(2,1)S(1)}, u32[]{:S(2)}, u32[]{:S(2)}) collective-permute-start(s16[200,512]{1,0:T(8,128)(2,1)S(1)} %get-tuple-element.60), channel_id=1, source_target_pairs={{0,24},{1,25},{2,26},{3,27},{4,7},{5,4},{6,5},{7,6},{8,0},{9,1},{1... | collective-permute-start | bytes 614408 | tf_op jit(solution)/shard_map/ppermute | solution.py:521
  51.9 4.9 %collective-permute-start.9 = (s16[104,512]{1,0:T(8,128)(2,1)S(1)}, s16[104,512]{1,0:T(8,128)(2,1)S(1)}, u32[]{:S(2)}, u32[]{:S(2)}) collective-permute-start(s16[104,512]{1,0:T(8,128)(2,1)S(1)} %get-tuple-element.63), channel_id=1, source_target_pairs={{0,32},{1,33},{2,34},{3,35},{4,228},{5,229},{6,230},{7,231},{8,40}... | collective-permute-start | bytes 319496 | tf_op jit(solution)/shard_map/ppermute | solution.py:521
  56.9 8.0 %collective-permute-start.10 = (s16[56,512]{1,0:T(8,128)(2,1)S(1)}, s16[56,512]{1,0:T(8,128)(2,1)S(1)}, u32[]{:S(2)}, u32[]{:S(2)}) collective-permute-start(s16[56,512]{1,0:T(8,128)(2,1)S(1)} %get-tuple-element.66), channel_id=1, source_target_pairs={{0,224},{1,225},{2,226},{3,227},{4,36},{5,37},{6,38},{7,39},{8,232... | collective-permute-start | bytes 172040 | tf_op jit(solution)/shard_map/ppermute | solution.py:521
  65.0 6.1 %collective-permute-start.11 = (s16[32,512]{1,0:T(8,128)(2,1)S(1)}, s16[32,512]{1,0:T(8,128)(2,1)S(1)}, u32[]{:S(2)}, u32[]{:S(2)}) collective-permute-start(s16[32,512]{1,0:T(8,128)(2,1)S(1)} %get-tuple-element.69), channel_id=1, source_target_pairs={{0,96},{1,97},{2,98},{3,99},{4,164},{5,165},{6,166},{7,167},{8,104... | collective-permute-start | bytes 98312 | tf_op jit(solution)/shard_map/ppermute | solution.py:521
